TPU v7x, 32 devices: a whole 2x2x4 slice. The times are simulated.
32 devices in a mesh: gx: 4 (over y, x), gy: 4 (over z), gz: 2 (over core).
Axes of the slice: x: 2, y: 2, z: 4, core: 2. Of those that a mesh axis runs over, the one named last changes fastest.
Arguments:
- correlators: bfloat16 [32, 32, 32, 16, 128], P(None, 'gx', 'gy', 'gz'), may hold values from -6 to 6
- momenta: int32 [125, 3], replicated, may hold values from -8 to 7
- source_channel: int32 [64], replicated, may hold values from 0 to 63
- phase_code: int32 [64], replicated, may hold values from 0 to 3
Outputs:
- projected: float32 [32, 125, 128], P('gx', None, ('gy', 'gz'))
All inputs are finite; a program needn't handle non-finite values.
Results may differ from a plain program's by a relative error of at most 0.002.
Values sent between devices are 32-bit elements; how exact they have to be, the bound alone decides.
A program may use at most 64 MiB of HBM per device.

v0:
```python
import math

import jax
import jax.numpy as jnp
from jax import lax
from jax.sharding import PartitionSpec as P


def axis_fraction(values, coords, extent):
    return jnp.mod(values[:, None] * coords[None, :], extent).astype(jnp.float32) / extent


def phase_table(momenta, coord_x, coord_y, coord_z, size_x, size_y, size_z):
    frac_x = axis_fraction(momenta[:, 0], coord_x, size_x)
    frac_y = axis_fraction(momenta[:, 1], coord_y, size_y)
    frac_z = axis_fraction(momenta[:, 2], coord_z, size_z)
    summed = frac_x[:, :, None, None] + frac_y[:, None, :, None]
    summed = summed + frac_z[:, None, None, :]
    angles = (summed * (2.0 * math.pi)).reshape(momenta.shape[0], -1)
    return jnp.concatenate([jnp.cos(angles), jnp.sin(angles)], axis=0).astype(jnp.bfloat16)


def channel_signs(phase_code):
    real_sign = jnp.where(phase_code == 0, 1.0, jnp.where(phase_code == 2, -1.0, 0.0)).astype(
        jnp.float32
    )
    imag_sign = jnp.where(phase_code == 1, 1.0, jnp.where(phase_code == 3, -1.0, 0.0)).astype(
        jnp.float32
    )
    return (real_sign, imag_sign)


def local(correlators, momenta, source_channel, phase_code):
    window, cells_x, cells_y, cells_z, width = correlators.shape
    channels = width // 2
    moment_count = momenta.shape[0]
    size_x = cells_x * lax.axis_size("gx")
    size_y = cells_y * lax.axis_size("gy")
    size_z = cells_z * lax.axis_size("gz")
    coord_x = lax.axis_index("gx") * cells_x + jnp.arange(cells_x, dtype=jnp.int32)
    coord_y = lax.axis_index("gy") * cells_y + jnp.arange(cells_y, dtype=jnp.int32)
    coord_z = lax.axis_index("gz") * cells_z + jnp.arange(cells_z, dtype=jnp.int32)
    phases = phase_table(momenta, coord_x, coord_y, coord_z, size_x, size_y, size_z)
    real_sign, imag_sign = channel_signs(phase_code)
    chosen = (jnp.arange(channels, dtype=jnp.int32)[:, None] == source_channel[None, :]).astype(
        jnp.float32
    )
    from_real = jnp.concatenate([chosen * real_sign[None, :], chosen * imag_sign[None, :]], axis=1)
    from_imag = jnp.concatenate([-chosen * imag_sign[None, :], chosen * real_sign[None, :]], axis=1)
    mixing = jnp.concatenate([from_real, from_imag], axis=0).astype(jnp.bfloat16)
    site_count = cells_x * cells_y * cells_z
    flat = correlators.reshape(window, site_count, width)
    norm_factor = 1.0 / math.sqrt(size_x * size_y * size_z)
    mixed = jnp.dot(flat.reshape(-1, width), mixing, preferred_element_type=jnp.float32)
    mixed = mixed.astype(jnp.bfloat16).reshape(window, site_count, width)
    product = jnp.einsum("ms,tsc->tmc", phases, mixed, preferred_element_type=jnp.float32)
    cos_part = product[:, :moment_count]
    sin_part = product[:, moment_count:]
    real_out = cos_part[:, :, :channels] + sin_part[:, :, channels:]
    imag_out = cos_part[:, :, channels:] - sin_part[:, :, :channels]
    partial_value = jnp.concatenate([real_out, imag_out], axis=2) * norm_factor
    summed = lax.psum_scatter(partial_value, ("gy", "gz"), scatter_dimension=2, tiled=True)
    return lax.psum_scatter(summed, "gx", scatter_dimension=0, tiled=True)


def solution(mesh):
    in_specs = (P(None, "gx", "gy", "gz", None), P(), P(), P())
    out_specs = P("gx", None, ("gy", "gz"))
    return jax.shard_map(local, mesh=mesh, in_specs=in_specs, out_specs=out_specs, check_vma=False)
```

profile of v0, /device:TPU:0, one launch (start us, length us, event | category | flops | bytes accessed | tf_op | source)
XLA Modules:
  0.0 90.0 jit_solution(3967452616583971880)
XLA Ops:
  6.5 0.0 reduce-scatter.3.cloned.1.call-start
  6.5 0.7 compare_select_fusion.1
  7.2 0.7 compare_select_fusion.3
  7.9 0.8 slice_bitcast_fusion.2
  8.7 0.7 multiply_convert_fusion
  9.3 0.7 select_convert_fusion
  10.0 0.1 fusion.20
  10.1 0.1 fusion.16
  10.2 1.0 %cosine_convert_fusion = (bf16[125,8,8,8]{0,3,2,1:T(8,128)(2,1)S(1)}, bf16[125,8,8,8]{0,3,2,1:T(8,128)(2,1)S(1)}) fusion(f32[125,8]{0,1:T(8,128)S(1)} %fusion.20, f32[125,8,8]{0,2,1:T(8,128)S(1)} %broadcast_add_fusion), kind=kLoop, calls=%fused_computation.12 | loop fusion | flops 256000 | bytes 292000 | tf_op jit(solution)/shard_map/convert.3
  11.2 0.1 copy.6
  11.3 0.1 copy.7
  11.5 3.5 %convolution_convert_fusion = bf16[128,16384]{1,0:T(8,128)(2,1)S(1)} fusion(bf16[16384,128]{1,0:T(8,128)(2,1)} %bitcast.23, bf16[64,64]{1,0:T(8,128)(2,1)S(1)} %get-tuple-element.13, bf16[64,64]{1,0:T(8,128)(2,1)S(1)} %multiply_convert_fusion, bf16[64,64]{1,0:T(8,128)(2,1)S(1)} %get-tuple-element.12), kind=kOutput, calls=%fused_computation | convolution fusion | flops 539099136 | bytes 8413184 | tf_op jit(solution)/shard_map/dot_general | solution.py:54
  15.0 1.3 %fusion.3 = f32[32,250,128]{1,2,0:T(8,128)S(1)} fusion(bf16[16,32,8,512]{3,2,1,0:T(8,128)(2,1)S(1)} %bitcast.22, bf16[125,512]{1,0:T(8,128)(2,1)S(1)} %copy.7, bf16[125,512]{1,0:T(8,128)(2,1)S(1)} %copy.6), kind=kOutput, calls=%fused_computation.4 | convolution fusion | flops 1049088000 | bytes 8546304 | tf_op jit(solution)/shard_map/ms,tsc->tmc/dot_general | solution.py:56
  16.3 0.6 slice_add_fusion
  16.9 1.6 %maximum_multiply_fusion = f32[32,125,128]{1,2,0:T(8,128)} fusion(f32[32,125,64]{1,2,0:T(8,128)S(1)} %get-tuple-element.6, f32[32,125,64]{1,2,0:T(8,128)S(1)} %get-tuple-element.5), kind=kLoop, calls=%fused_computation.5 | loop fusion | flops 1024000 | bytes 4096000 | tf_op jit(solution)/shard_map/mul | solution.py:61
  18.5 0.0 reduce-scatter.3.cloned.1.call-update
  18.5 0.0 reduce-scatter.5.cloned.1.call-start
  18.6 38.9 %reduce-scatter.3.cloned.1.call-done = f32[32,125,16]{1,2,0:T(8,128)} async-done(((f32[32,125,128]{1,2,0:T(8,128)}), f32[32,125,16]{1,2,0:T(8,128)}) %reduce-scatter.3.cloned.1.call-update) | async-done | bytes 256016 | tf_op jit(solution)/shard_map/reduce_scatter | solution.py:62
  57.5 0.0 reduce-scatter.5.cloned.1.call-update
  57.5 25.6 %reduce-scatter.5.cloned.1.call-done = f32[8,125,16]{1,2,0:T(8,128)} async-done(((f32[32,125,16]{1,2,0:T(8,128)}), f32[8,125,16]{1,2,0:T(8,128)}) %reduce-scatter.5.cloned.1.call-update) | async-done | bytes 64016 | tf_op jit(solution)/shard_map/reduce_scatter | solution.py:63
  (4 shorter events, 0.0 us)
Async XLA Ops:
  6.5 50.9 %reduce-scatter.3.cloned.1.call-start = ((), (), s32[]{:S(2)}) async-start(), calls=%async_computation.2 | async-start | bytes 2359296 | tf_op jit(solution)/shard_map/reduce_scatter | solution.py:62
  18.5 64.6 %reduce-scatter.5.cloned.1.call-start = ((), (), s32[]{:S(2)}) async-start(), calls=%async_computation.3 | async-start | bytes 327680 | tf_op jit(solution)/shard_map/reduce_scatter | solution.py:63
Sparse Core Ops, SparseCore 0:
  18.7 38.7 reduce-scatter.2
  60.2 22.8 reduce-scatter.4
where the time goes:
time: 90.2 us; the launch traced here: 90 us
  waiting for transfers between devices  64.5 us (72%)
  between operations  13.4 us (15%)
  other arithmetic  6.01 us (7%)
  matrix products  4.84 us (5%)
  local copies, waits for them, and re-layouts  1.08 us (1%)
    reduce_scatter x1, waiting for transfers between devices, local(): lax.psum_scatter(partial_value, ('gy', 'gz'), scatter_dimension=2, tiled=...  38.9 us
    reduce_scatter x1, waiting for transfers between devices, local(): return lax.psum_scatter(summed, 'gx', scatter_dimension=0, tiled=True)  25.6 us
    dot_general x1, matrix products, local(): jnp.dot(flat.reshape(-1, width), mixing, preferred_element_type=jnp.float32)  3.54 us
    another operation x3, other arithmetic  2.33 us
  transfers between devices with their start and end apart: 2, of which 2 were waited for; matrix products, arithmetic and copies ran while one was open for 0% of the time, Pallas kernels for 0%

commit v1 on v0

v1 whole, which is shorter than its diff:
```python
import functools
import math

import jax
import jax.numpy as jnp
from jax import lax
from jax.experimental import pallas as pl
from jax.experimental.pallas import tpu as pltpu
from jax.sharding import PartitionSpec as P

LANES = 128
SUBLANES = 8
HALVES = 2


def round_up(value, unit):
    return (value + unit - 1) // unit * unit


def kernel(dims, corr, momenta, source, code, out, *scratch):
    (nx, ny, nz, na, nb, tpo, chunks, cells, sites, width, mom, cb, cbp, norm) = dims
    (raw, table, phases, part, got_a, send_b1, got_b1, send_b2, got_b2, send_c, got_c,
     load_sem, sa, ra, sb1, rb1, sb2, rb2, sc, rc) = scratch
    cells_x, cells_y, cells_z = cells
    lanes = table.shape[1]
    channels = width // 2
    rows = ny * cbp
    me_x, me_y, me_z = lax.axis_index("gx"), lax.axis_index("gy"), lax.axis_index("gz")
    me_a, me_b = me_x // nb, lax.rem(me_x, nb)

    loads = {}
    for j in range(chunks):
        for g in range(nx):
            at = pl.ds(g * tpo + j * HALVES, HALVES)
            loads[j, g] = pltpu.make_async_copy(corr.at[at], raw.at[at], load_sem.at[j, g])
            loads[j, g].start()

    def at_z(o):
        return {"gz": lax.rem(me_z + o, nz)}

    def at_a(o):
        return {"gx": lax.rem(me_a + o, na) * nb + me_b}

    def at_b(o):
        return {"gx": me_a * nb + lax.rem(me_b + o, nb)}

    def at_y(o):
        return {"gy": lax.rem(me_y + o, ny)}

    partners = [at_z(o) for o in range(1, nz)] + [at_a(o) for o in range(1, na)]
    partners += [at_b(o) for o in range(1, nb)] + [at_y(o) for o in range(1, ny)]
    barrier = pltpu.get_barrier_semaphore()
    for where in partners:
        pl.semaphore_signal(barrier, inc=1, device_id=where, device_id_type=pl.DeviceIdType.MESH)

    table[...] = jnp.zeros_like(table)
    table[0:3, 0:mom] = momenta[...]
    ks = table[...].astype(jnp.float32)

    def axis_table(axis, count, offset, extent):
        coord = lax.broadcasted_iota(jnp.int32, (count, lanes), 0) + offset
        turns = ks[axis:axis + 1, :] * coord.astype(jnp.float32) * (1.0 / extent)
        angle = (turns - jnp.floor(turns)) * (2.0 * math.pi)
        return jnp.cos(angle), jnp.sin(angle)

    cx, sx = axis_table(0, cells_x, me_x * cells_x, cells_x * nx)
    cy, sy = axis_table(1, cells_y, me_y * cells_y, cells_y * ny)
    cz, sz = axis_table(2, cells_z, me_z * cells_z, cells_z * nz)
    for x in range(cells_x):
        cxx, sxx = cx[x:x + 1], sx[x:x + 1]
        cxy, sxy = cxx * cy - sxx * sy, sxx * cy + cxx * sy
        for y in range(cells_y):
            c1, s1 = cxy[y:y + 1], sxy[y:y + 1]
            at = (x * cells_y + y) * cells_z
            phases[at:at + cells_z, 0:lanes] = (c1 * cz - s1 * sz).astype(phases.dtype)
            phases[at:at + cells_z, lanes:] = (s1 * cz + c1 * sz).astype(phases.dtype)

    total_rows = nz * rows
    row = lax.broadcasted_iota(jnp.int32, (total_rows, channels), 0)
    lane = lax.broadcasted_iota(jnp.int32, (total_rows, channels), 1)
    row_z, row_y, row_r = row // rows, (row % rows) // cbp, row % cbp
    channel = (row_y * nz + row_z) * cb + row_r
    is_imag = channel >= channels
    picked = lane == jnp.where(is_imag, channel - channels, channel)
    src = jnp.sum(jnp.where(picked, source[...].astype(jnp.float32), 0.0), axis=1, keepdims=True)
    cod = jnp.sum(jnp.where(picked, code[...].astype(jnp.float32), 0.0), axis=1, keepdims=True)
    row = lax.broadcasted_iota(jnp.int32, (total_rows, width), 0)
    k = lax.broadcasted_iota(jnp.int32, (total_rows, width), 1)
    row_z, row_y, row_r = row // rows, (row % rows) // cbp, row % cbp
    is_imag = (row_y * nz + row_z) * cb + row_r >= channels
    from_imag = k >= channels
    quarter = cod + jnp.where(from_imag, 1.0, 0.0) + jnp.where(is_imag, 3.0, 0.0)
    sign = jnp.where((quarter == 0.0) | (quarter == 4.0), 1.0, 0.0)
    sign = sign - jnp.where((quarter == 2.0) | (quarter == 6.0), 1.0, 0.0)
    hit = (jnp.where(from_imag, k - channels, k).astype(jnp.float32) == src) & (row_r < cb)
    mixing = jnp.where(hit, sign, 0.0).astype(jnp.bfloat16)

    def compute(j):
        for g in range(nx):
            loads[j, g].wait()
            first = g * tpo + j * HALVES
            block = raw[first:first + HALVES].reshape(HALVES * sites, width)
            mixed = lax.dot_general(
                mixing, block, (((1,), (1,)), ((), ())), preferred_element_type=jnp.float32
            ).astype(jnp.bfloat16)
            stacked = jnp.concatenate(
                [mixed[:, u * sites:(u + 1) * sites] for u in range(HALVES)], axis=0
            )
            product = jnp.dot(stacked, phases[...], preferred_element_type=jnp.float32)
            for u in range(HALVES):
                order = g // nb, g % nb
                place = order[1] * na + order[0] if u == 0 else g
                for z in range(nz):
                    at = u * total_rows + z * rows
                    mid = at + rows // 2
                    re, im = product[at:mid], product[mid:at + rows]
                    part[j, z, u, place, 0:rows // 2] = re[:, :lanes] + im[:, lanes:]
                    part[j, z, u, place, rows // 2:] = im[:, :lanes] - re[:, lanes:]

    def remote(src_ref, dst_ref, send, recv, where):
        return pltpu.make_async_remote_copy(
            src_ref=src_ref, dst_ref=dst_ref, send_sem=send, recv_sem=recv,
            device_id=where, device_id_type=pl.DeviceIdType.MESH,
        )

    sent = []
    a_copies, b1_copies, b2_copies, c_copies = {}, {}, {}, {}
    lead = (nb, na)
    trail = (na, nb)
    me_lead = (me_b, me_a)
    me_trail = (me_a, me_b)
    at_lead = (at_b, at_a)
    at_trail = (at_a, at_b)

    def send_stage_a(j):
        for o in range(1, nz):
            copy = remote(part.at[j, lax.rem(me_z + o, nz)], got_a.at[j, o - 1],
                          sa.at[j, o - 1], ra.at[j, o - 1], at_z(o))
            copy.start()
            a_copies.setdefault(j, []).append(copy)
            sent.append(copy)

    def sum_a(j, u, place):
        value = part[j, me_z, u, place]
        for o in range(nz - 1):
            value = value + got_a[j, o, u, place]
        return value

    def stage_b1(j):
        for copy in a_copies[j]:
            copy.wait_recv()
        for u in range(HALVES):
            for o in range(1, lead[u]):
                target = lax.rem(me_lead[u] + o, lead[u])
                for i in range(trail[u]):
                    send_b1[u][j, o - 1, i] = sum_a(j, u, target * trail[u] + i)
                copy = remote(send_b1[u].at[j, o - 1], got_b1[u].at[j, o - 1],
                              sb1[u].at[j, o - 1], rb1[u].at[j, o - 1], at_lead[u](o))
                copy.start()
                b1_copies.setdefault((j, u), []).append(copy)
                sent.append(copy)

    def sum_b1(j, u, i):
        value = sum_a(j, u, me_lead[u] * trail[u] + i)
        for o in range(lead[u] - 1):
            value = value + got_b1[u][j, o, i]
        return value

    def stage_b2(j):
        for u in range(HALVES):
            for copy in b1_copies.get((j, u), []):
                copy.wait_recv()
            for o in range(1, trail[u]):
                target = lax.rem(me_trail[u] + o, trail[u])
                send_b2[u][j, o - 1] = sum_b1(j, u, target)
                copy = remote(send_b2[u].at[j, o - 1], got_b2[u].at[j, o - 1],
                              sb2[u].at[j, o - 1], rb2[u].at[j, o - 1], at_trail[u](o))
                copy.start()
                b2_copies.setdefault((j, u), []).append(copy)
                sent.append(copy)

    def stage_c(j):
        for u in range(HALVES):
            for copy in b2_copies.get((j, u), []):
                copy.wait_recv()
            value = sum_b1(j, u, me_trail[u])
            for o in range(trail[u] - 1):
                value = value + got_b2[u][j, o]
            for y in range(ny):
                send_c[j, y, u] = value[y * cbp:(y + 1) * cbp]
        for o in range(1, ny):
            copy = remote(send_c.at[j, lax.rem(me_y + o, ny)], got_c.at[j, o - 1],
                          sc.at[j, o - 1], rc.at[j, o - 1], at_y(o))
            copy.start()
            c_copies.setdefault(j, []).append(copy)
            sent.append(copy)

    def finish(j):
        for copy in c_copies.get(j, []):
            copy.wait_recv()
        for u in range(HALVES):
            value = send_c[j, me_y, u]
            for o in range(ny - 1):
                value = value + got_c[j, o, u]
            out[j * HALVES + u] = (value * norm)[:, :mom]

    compute(0)
    pl.semaphore_wait(barrier, len(partners))
    send_stage_a(0)
    stages = (stage_b1, stage_b2, stage_c, finish)
    for step in range(1, chunks + len(stages)):
        if step < chunks:
            compute(step)
            send_stage_a(step)
        for depth, stage in enumerate(stages):
            j = step - 1 - depth
            if 0 <= j < chunks:
                stage(j)
    for copy in sent:
        copy.wait_send()


def local(axis_sizes, correlators, momenta, source_channel, phase_code):
    nx, ny, nz = axis_sizes
    window, cells_x, cells_y, cells_z, width = correlators.shape
    mom = momenta.shape[0]
    nb = 2 if nx % 2 == 0 else 1
    na = nx // nb
    tpo = window // nx
    chunks = tpo // HALVES
    cb = width // (ny * nz)
    cbp = round_up(cb, SUBLANES)
    rows = ny * cbp
    sites = cells_x * cells_y * cells_z
    lanes = round_up(mom, LANES)
    norm = 1.0 / math.sqrt(sites * nx * ny * nz)
    dims = (nx, ny, nz, na, nb, tpo, chunks, (cells_x, cells_y, cells_z), sites, width, mom, cb, cbp, norm)

    def buffer(*shape):
        return pltpu.VMEM(shape, jnp.float32)

    def sems(*shape):
        return pltpu.SemaphoreType.DMA(shape)

    def less(count):
        return max(count - 1, 1)

    lead, trail = (nb, na), (na, nb)
    scratch = [
        pltpu.VMEM((window, sites, width), correlators.dtype),
        pltpu.VMEM((SUBLANES, lanes), jnp.int32),
        pltpu.VMEM((sites, 2 * lanes), jnp.bfloat16),
        buffer(chunks, nz, HALVES, nx, rows, lanes),
        buffer(chunks, less(nz), HALVES, nx, rows, lanes),
        [buffer(chunks, less(lead[u]), trail[u], rows, lanes) for u in range(HALVES)],
        [buffer(chunks, less(lead[u]), trail[u], rows, lanes) for u in range(HALVES)],
        [buffer(chunks, less(trail[u]), rows, lanes) for u in range(HALVES)],
        [buffer(chunks, less(trail[u]), rows, lanes) for u in range(HALVES)],
        buffer(chunks, ny, HALVES, cbp, lanes),
        buffer(chunks, less(ny), HALVES, cbp, lanes),
        sems(chunks, nx),
        sems(chunks, less(nz)),
        sems(chunks, less(nz)),
        [sems(chunks, less(lead[u])) for u in range(HALVES)],
        [sems(chunks, less(lead[u])) for u in range(HALVES)],
        [sems(chunks, less(trail[u])) for u in range(HALVES)],
        [sems(chunks, less(trail[u])) for u in range(HALVES)],
        sems(chunks, less(ny)),
        sems(chunks, less(ny)),
    ]
    vmem = pl.BlockSpec(memory_space=pltpu.VMEM)
    result = pl.pallas_call(
        functools.partial(kernel, dims),
        out_shape=jax.ShapeDtypeStruct((tpo, cbp, mom), jnp.float32),
        in_specs=[pl.BlockSpec(memory_space=pl.ANY), vmem, vmem, vmem],
        out_specs=vmem,
        scratch_shapes=scratch,
        compiler_params=pltpu.CompilerParams(
            collective_id=0, has_side_effects=True, vmem_limit_bytes=48 * 1024 * 1024
        ),
        name="project",
    )(
        correlators.reshape(window, sites, width),
        momenta.T,
        source_channel.reshape(1, -1),
        phase_code.reshape(1, -1),
    )
    return jnp.swapaxes(result[:, :cb], 1, 2)


def solution(mesh):
    axis_sizes = tuple(mesh.shape[name] for name in ("gx", "gy", "gz"))
    in_specs = (P(None, "gx", "gy", "gz", None), P(), P(), P())
    out_specs = P("gx", None, ("gy", "gz"))
    return jax.shard_map(
        functools.partial(local, axis_sizes),
        mesh=mesh, in_specs=in_specs, out_specs=out_specs, check_vma=False,
    )
```

time: 90.2 us -> 30.9 us (0.34)
  waiting for transfers between devices: 64.5 us -> 0 us
  Pallas kernels: 0 us -> 25.9 us
  between operations: 13.4 us -> 0.01 us
  other arithmetic: 6.01 us -> 0 us
  matrix products: 4.84 us -> 0 us
  local copies, waits for them, and re-layouts: 1.08 us -> 4.81 us
    reduce_scatter x2 -> x0, waiting for transfers between devices: 64.5 us -> none  [the longest x1 38.9 us: local(): lax.psum_scatter(partial_value, ('gy', 'gz'), scatter_dimension=2, tiled=...]
    pallas_call x0 -> x1, Pallas kernels: none -> 25.9 us  [local(): pl.pallas_call(functools.partial(kernel, dims), out_shape=jax.ShapeDtypeS...]
    dot_general x2 -> x0, matrix products: 4.84 us -> none  [the longest x1 3.54 us: local(): jnp.dot(flat.reshape(-1, width), mixing, preferred_element_type=jnp.float32)]
    unnamed x0 -> x9, local copies, waits for them, and re-layouts: none -> 4.81 us
    another operation x3 -> x0, other arithmetic: 2.33 us -> none
    mul x1 -> x0, other arithmetic: 1.58 us -> none  [local(): partial_value = jnp.concatenate([real_out, imag_out], axis=2) * norm_factor]
    select_n x2 -> x0, other arithmetic: 1.32 us -> none  [the longest x1 0.66 us: channel_signs(): jnp.where(phase_code == 0, 1.0, jnp.where(phase_code == 2, -1.0, 0.0))]
  transfers between devices with their start and end apart: 2 -> 0, of which waited for: 2 -> 0; matrix products, arithmetic and copies ran while one was open for 0% -> 0% of each run, Pallas kernels for 0% -> 0%
where the time goes in v1:
time: 30.9 us; the launch traced here: 30.8 us
  Pallas kernels  25.9 us (84%)
  local copies, waits for them, and re-layouts  4.81 us (16%)
    pallas_call x1, Pallas kernels, local(): pl.pallas_call(functools.partial(kernel, dims), out_shape=jax.ShapeDtypeS...  25.9 us
    unnamed x9, local copies, waits for them, and re-layouts  4.81 us

profile of v1, /device:TPU:0, one launch (start us, length us, event | category | flops | bytes accessed | tf_op | source)
XLA Modules:
  0.0 30.8 jit_solution(9417254855697960120)
XLA Ops:
  0.0 0.0 copy-start
  0.0 2.2 %copy-done = bf16[32,8,8,8,128]{4,3,2,1,0:T(8,128)(2,1)S(1)} copy-done((bf16[32,8,8,8,128]{4,3,2,1,0:T(8,128)(2,1)S(1)}, bf16[32,8,8,8,128]{4,3,2,1,0:T(8,128)(2,1)}, u32[]{:S(2)}) %copy-start) | copy-done | bytes 4194328
  2.2 0.0 copy-start.1
  2.2 0.7 %copy-done.1 = s32[125,3]{0,1:T(4,128)S(1)} copy-done((s32[125,3]{0,1:T(4,128)S(1)}, s32[125,3]{0,1:T(4,128)}, u32[]{:S(2)}) %copy-start.1) | copy-done | bytes 1524
  2.9 0.0 copy-start.2
  2.9 0.7 %copy-done.2 = s32[64]{0:T(128)S(1)} copy-done((s32[64]{0:T(128)S(1)}, s32[64]{0:T(128)}, u32[]{:S(2)}) %copy-start.2) | copy-done | bytes 280
  3.5 0.0 copy-start.3
  3.5 0.7 %copy-done.3 = s32[64]{0:T(128)S(1)} copy-done((s32[64]{0:T(128)S(1)}, s32[64]{0:T(128)}, u32[]{:S(2)}) %copy-start.3) | copy-done | bytes 280
  4.2 25.9 %project.1 = f32[8,16,125]{2,1,0:T(8,128)S(1)} custom-call(bf16[32,512,128]{2,1,0:T(8,128)(2,1)S(1)} %bitcast.5, s32[3,125]{1,0:T(4,128)S(1)} %bitcast.7, s32[1,64]{1,0:T(1,128)S(1)} %bitcast.8, s32[1,64]{1,0:T(1,128)S(1)} %bitcast.9), custom_call_target="tpu_custom_call" | custom-call | tf_op jit(solution)/shard_map/project/pallas_call | solution.py:272
  30.1 0.6 %copy.6 = f32[8,125,16]{1,2,0:T(8,128)} copy(f32[8,125,16]{1,2,0:T(8,128)S(1)} %bitcast.6) | data formatting | bytes 128000
Async XLA Ops:
  0.0 2.2 %copy-start = (bf16[32,8,8,8,128]{4,3,2,1,0:T(8,128)(2,1)S(1)}, bf16[32,8,8,8,128]{4,3,2,1,0:T(8,128)(2,1)}, u32[]{:S(2)}) copy-start(bf16[32,8,8,8,128]{4,3,2,1,0:T(8,128)(2,1)} %param.4) | copy-start | bytes 12582916
  2.2 0.7 %copy-start.1 = (s32[125,3]{0,1:T(4,128)S(1)}, s32[125,3]{0,1:T(4,128)}, u32[]{:S(2)}) copy-start(s32[125,3]{0,1:T(4,128)} %param.5) | copy-start | bytes 4504
  2.9 0.7 %copy-start.2 = (s32[64]{0:T(128)S(1)}, s32[64]{0:T(128)}, u32[]{:S(2)}) copy-start(s32[64]{0:T(128)} %param.6) | copy-start | bytes 772
  3.5 0.7 %copy-start.3 = (s32[64]{0:T(128)S(1)}, s32[64]{0:T(128)}, u32[]{:S(2)}) copy-start(s32[64]{0:T(128)} %param.7) | copy-start | bytes 772

commit v2 on v1

--- a/solution.py
+++ b/solution.py
@@ -17,12 +17,12 @@
     return (value + unit - 1) // unit * unit
 
 
-def kernel(dims, corr, momenta, source, code, out, *scratch):
+def kernel(dims, corr, small, out, *scratch):
     (nx, ny, nz, na, nb, tpo, chunks, cells, sites, width, mom, cb, cbp, norm) = dims
-    (raw, table, phases, part, got_a, send_b1, got_b1, send_b2, got_b2, send_c, got_c,
+    (raw, phases, part, got_a, send_b1, got_b1, send_b2, got_b2, send_c, got_c,
      load_sem, sa, ra, sb1, rb1, sb2, rb2, sc, rc) = scratch
     cells_x, cells_y, cells_z = cells
-    lanes = table.shape[1]
+    lanes = phases.shape[1] // 2
     channels = width // 2
     rows = ny * cbp
     me_x, me_y, me_z = lax.axis_index("gx"), lax.axis_index("gy"), lax.axis_index("gz")
@@ -53,9 +53,8 @@
     for where in partners:
         pl.semaphore_signal(barrier, inc=1, device_id=where, device_id_type=pl.DeviceIdType.MESH)
 
-    table[...] = jnp.zeros_like(table)
-    table[0:3, 0:mom] = momenta[...]
-    ks = table[...].astype(jnp.float32)
+    ks = small[0:3, 0:lanes].astype(jnp.float32)
+    source, code = small[3:4, 0:width // 2], small[4:5, 0:width // 2]
 
     def axis_table(axis, count, offset, extent):
         coord = lax.broadcasted_iota(jnp.int32, (count, lanes), 0) + offset
@@ -82,8 +81,8 @@
     channel = (row_y * nz + row_z) * cb + row_r
     is_imag = channel >= channels
     picked = lane == jnp.where(is_imag, channel - channels, channel)
-    src = jnp.sum(jnp.where(picked, source[...].astype(jnp.float32), 0.0), axis=1, keepdims=True)
-    cod = jnp.sum(jnp.where(picked, code[...].astype(jnp.float32), 0.0), axis=1, keepdims=True)
+    src = jnp.sum(jnp.where(picked, source.astype(jnp.float32), 0.0), axis=1, keepdims=True)
+    cod = jnp.sum(jnp.where(picked, code.astype(jnp.float32), 0.0), axis=1, keepdims=True)
     row = lax.broadcasted_iota(jnp.int32, (total_rows, width), 0)
     k = lax.broadcasted_iota(jnp.int32, (total_rows, width), 1)
     row_z, row_y, row_r = row // rows, (row % rows) // cbp, row % cbp
@@ -236,6 +235,12 @@
     norm = 1.0 / math.sqrt(sites * nx * ny * nz)
     dims = (nx, ny, nz, na, nb, tpo, chunks, (cells_x, cells_y, cells_z), sites, width, mom, cb, cbp, norm)
 
+    small_lanes = max(lanes, round_up(width // 2, LANES))
+    small = sum(
+        jnp.pad(row, ((at, SUBLANES - at - row.shape[0]), (0, small_lanes - row.shape[1])))
+        for at, row in ((0, momenta.T), (3, source_channel[None]), (4, phase_code[None]))
+    )
+
     def buffer(*shape):
         return pltpu.VMEM(shape, jnp.float32)
 
@@ -248,7 +253,6 @@
     lead, trail = (nb, na), (na, nb)
     scratch = [
         pltpu.VMEM((window, sites, width), correlators.dtype),
-        pltpu.VMEM((SUBLANES, lanes), jnp.int32),
         pltpu.VMEM((sites, 2 * lanes), jnp.bfloat16),
         buffer(chunks, nz, HALVES, nx, rows, lanes),
         buffer(chunks, less(nz), HALVES, nx, rows, lanes),
@@ -268,22 +272,20 @@
         sems(chunks, less(ny)),
         sems(chunks, less(ny)),
     ]
-    vmem = pl.BlockSpec(memory_space=pltpu.VMEM)
+    vmem, hbm = pl.BlockSpec(memory_space=pltpu.VMEM), pl.BlockSpec(memory_space=pltpu.HBM)
     result = pl.pallas_call(
         functools.partial(kernel, dims),
         out_shape=jax.ShapeDtypeStruct((tpo, cbp, mom), jnp.float32),
-        in_specs=[pl.BlockSpec(memory_space=pl.ANY), vmem, vmem, vmem],
+        in_specs=[hbm, vmem],
         out_specs=vmem,
         scratch_shapes=scratch,
         compiler_params=pltpu.CompilerParams(
-            collective_id=0, has_side_effects=True, vmem_limit_bytes=48 * 1024 * 1024
+            collective_id=0, has_side_effects=True, vmem_limit_bytes=52 * 1024 * 1024
         ),
         name="project",
     )(
         correlators.reshape(window, sites, width),
-        momenta.T,
-        source_channel.reshape(1, -1),
-        phase_code.reshape(1, -1),
+        small,
     )
     return jnp.swapaxes(result[:, :cb], 1, 2)
 

time: 30.9 us -> 27.3 us (0.88)
  local copies, waits for them, and re-layouts: 4.81 us -> 0.63 us
  other arithmetic: 0 us -> 0.72 us
    unnamed x9 -> x1, local copies, waits for them, and re-layouts: 4.81 us -> 0.63 us
    add x0 -> x1, other arithmetic: none -> 0.72 us  [local(): sum((jnp.pad(row, ((at, SUBLANES - at - row.shape[0]), (0, small_lanes -...]
where the time goes in v2:
time: 27.3 us; the launch traced here: 27.1 us
  Pallas kernels  25.8 us (95%)
  other arithmetic  0.72 us (3%)
  local copies, waits for them, and re-layouts  0.63 us (2%)
    pallas_call x1, Pallas kernels, local(): pl.pallas_call(functools.partial(kernel, dims), out_shape=jax.ShapeDtypeS...  25.8 us
    add x1, other arithmetic, local(): sum((jnp.pad(row, ((at, SUBLANES - at - row.shape[0]), (0, small_lanes -...  0.72 us
    unnamed x1, local copies, waits for them, and re-layouts  0.63 us

profile of v2, /device:TPU:0, one launch (start us, length us, event | category | flops | bytes accessed | tf_op | source)
XLA Modules:
  0.0 27.1 jit_solution(4602050353655198495)
XLA Ops:
  0.0 0.7 %pad_add_fusion.small = s32[8,128]{1,0:T(8,128)S(1)} fusion(s32[1,64]{1,0:T(1,128)} %bitcast.8, s32[1,64]{1,0:T(1,128)} %bitcast.9, s32[3,125]{1,0:T(4,128)} %bitcast.7), kind=kLoop, calls=%fused_computation | loop fusion | flops 2048 | bytes 6108 | tf_op jit(solution)/shard_map/add | solution.py:239
  0.7 25.8 %project.1 = f32[8,16,125]{2,1,0:T(8,128)S(1)} custom-call(bf16[32,512,128]{2,1,0:T(8,128)(2,1)} %bitcast.6, s32[8,128]{1,0:T(8,128)S(1)} %pad_add_fusion.small), custom_call_target="tpu_custom_call" | custom-call | tf_op jit(solution)/shard_map/project/pallas_call | solution.py:276
  26.5 0.6 %copy.6 = f32[8,125,16]{1,2,0:T(8,128)} copy(f32[8,125,16]{1,2,0:T(8,128)S(1)} %bitcast.5) | data formatting | bytes 128000

commit v3 on v2

--- a/solution.py
+++ b/solution.py
@@ -11,6 +11,8 @@
 LANES = 128
 SUBLANES = 8
 HALVES = 2
+LAGS = (1, 4, 7, 10)
+GROUP = 4
 
 
 def round_up(value, unit):
@@ -25,15 +27,18 @@
     lanes = phases.shape[1] // 2
     channels = width // 2
     rows = ny * cbp
+    half_rows = rows // HALVES
     me_x, me_y, me_z = lax.axis_index("gx"), lax.axis_index("gy"), lax.axis_index("gz")
     me_a, me_b = me_x // nb, lax.rem(me_x, nb)
 
-    loads = {}
-    for j in range(chunks):
+    def load(j, g):
+        at = g * tpo + j
+        return pltpu.make_async_copy(corr.at[at], raw.at[at], load_sem.at[j, g])
+
+    @pl.loop(0, chunks)
+    def _(j):
         for g in range(nx):
-            at = pl.ds(g * tpo + j * HALVES, HALVES)
-            loads[j, g] = pltpu.make_async_copy(corr.at[at], raw.at[at], load_sem.at[j, g])
-            loads[j, g].start()
+            load(j, g).start()
 
     def at_z(o):
         return {"gz": lax.rem(me_z + o, nz)}
@@ -95,26 +100,25 @@
     mixing = jnp.where(hit, sign, 0.0).astype(jnp.bfloat16)
 
     def compute(j):
-        for g in range(nx):
-            loads[j, g].wait()
-            first = g * tpo + j * HALVES
-            block = raw[first:first + HALVES].reshape(HALVES * sites, width)
-            mixed = lax.dot_general(
-                mixing, block, (((1,), (1,)), ((), ())), preferred_element_type=jnp.float32
-            ).astype(jnp.bfloat16)
-            stacked = jnp.concatenate(
-                [mixed[:, u * sites:(u + 1) * sites] for u in range(HALVES)], axis=0
-            )
+        for first in range(0, nx, GROUP):
+            owners = range(first, min(first + GROUP, nx))
+            stacked = []
+            for g in owners:
+                load(j, g).wait()
+                stacked.append(lax.dot_general(
+                    mixing, raw[g * tpo + j], (((1,), (1,)), ((), ())),
+                    preferred_element_type=jnp.float32,
+                ).astype(jnp.bfloat16))
+            stacked = jnp.concatenate(stacked, axis=0)
             product = jnp.dot(stacked, phases[...], preferred_element_type=jnp.float32)
-            for u in range(HALVES):
-                order = g // nb, g % nb
-                place = order[1] * na + order[0] if u == 0 else g
+            for g in owners:
                 for z in range(nz):
-                    at = u * total_rows + z * rows
-                    mid = at + rows // 2
+                    at = (g - first) * total_rows + z * rows
+                    mid = at + half_rows
                     re, im = product[at:mid], product[mid:at + rows]
-                    part[j, z, u, place, 0:rows // 2] = re[:, :lanes] + im[:, lanes:]
-                    part[j, z, u, place, rows // 2:] = im[:, :lanes] - re[:, lanes:]
+                    place = (g % nb) * na + g // nb
+                    part[j, z, 0, place] = re[:, :lanes] + im[:, lanes:]
+                    part[j, z, 1, g] = im[:, :lanes] - re[:, lanes:]
 
     def remote(src_ref, dst_ref, send, recv, where):
         return pltpu.make_async_remote_copy(
@@ -122,8 +126,6 @@
             device_id=where, device_id_type=pl.DeviceIdType.MESH,
         )
 
-    sent = []
-    a_copies, b1_copies, b2_copies, c_copies = {}, {}, {}, {}
     lead = (nb, na)
     trail = (na, nb)
     me_lead = (me_b, me_a)
@@ -131,13 +133,25 @@
     at_lead = (at_b, at_a)
     at_trail = (at_a, at_b)
 
+    def a_copies(j):
+        return [remote(part.at[j, lax.rem(me_z + o, nz)], got_a.at[j, o - 1],
+                       sa.at[j, o - 1], ra.at[j, o - 1], at_z(o)) for o in range(1, nz)]
+
+    def b1_copies(j, u):
+        return [remote(send_b1[u].at[j, o - 1], got_b1[u].at[j, o - 1], sb1[u].at[j, o - 1],
+                       rb1[u].at[j, o - 1], at_lead[u](o)) for o in range(1, lead[u])]
+
+    def b2_copies(j, u):
+        return [remote(send_b2[u].at[j, o - 1], got_b2[u].at[j, o - 1], sb2[u].at[j, o - 1],
+                       rb2[u].at[j, o - 1], at_trail[u](o)) for o in range(1, trail[u])]
+
+    def c_copies(j):
+        return [remote(send_c.at[j, lax.rem(me_y + o, ny)], got_c.at[j, o - 1],
+                       sc.at[j, o - 1], rc.at[j, o - 1], at_y(o)) for o in range(1, ny)]
+
     def send_stage_a(j):
-        for o in range(1, nz):
-            copy = remote(part.at[j, lax.rem(me_z + o, nz)], got_a.at[j, o - 1],
-                          sa.at[j, o - 1], ra.at[j, o - 1], at_z(o))
+        for copy in a_copies(j):
             copy.start()
-            a_copies.setdefault(j, []).append(copy)
-            sent.append(copy)
 
     def sum_a(j, u, place):
         value = part[j, me_z, u, place]
@@ -146,18 +160,14 @@
         return value
 
     def stage_b1(j):
-        for copy in a_copies[j]:
+        for copy in a_copies(j):
             copy.wait_recv()
         for u in range(HALVES):
-            for o in range(1, lead[u]):
-                target = lax.rem(me_lead[u] + o, lead[u])
+            for o, copy in enumerate(b1_copies(j, u)):
+                target = lax.rem(me_lead[u] + o + 1, lead[u])
                 for i in range(trail[u]):
-                    send_b1[u][j, o - 1, i] = sum_a(j, u, target * trail[u] + i)
-                copy = remote(send_b1[u].at[j, o - 1], got_b1[u].at[j, o - 1],
-                              sb1[u].at[j, o - 1], rb1[u].at[j, o - 1], at_lead[u](o))
+                    send_b1[u][j, o, i] = sum_a(j, u, target * trail[u] + i)
                 copy.start()
-                b1_copies.setdefault((j, u), []).append(copy)
-                sent.append(copy)
 
     def sum_b1(j, u, i):
         value = sum_a(j, u, me_lead[u] * trail[u] + i)
@@ -167,56 +177,53 @@
 
     def stage_b2(j):
         for u in range(HALVES):
-            for copy in b1_copies.get((j, u), []):
+            for copy in b1_copies(j, u):
                 copy.wait_recv()
-            for o in range(1, trail[u]):
-                target = lax.rem(me_trail[u] + o, trail[u])
-                send_b2[u][j, o - 1] = sum_b1(j, u, target)
-                copy = remote(send_b2[u].at[j, o - 1], got_b2[u].at[j, o - 1],
-                              sb2[u].at[j, o - 1], rb2[u].at[j, o - 1], at_trail[u](o))
+            for o, copy in enumerate(b2_copies(j, u)):
+                send_b2[u][j, o] = sum_b1(j, u, lax.rem(me_trail[u] + o + 1, trail[u]))
                 copy.start()
-                b2_copies.setdefault((j, u), []).append(copy)
-                sent.append(copy)
 
     def stage_c(j):
         for u in range(HALVES):
-            for copy in b2_copies.get((j, u), []):
+            for copy in b2_copies(j, u):
                 copy.wait_recv()
             value = sum_b1(j, u, me_trail[u])
             for o in range(trail[u] - 1):
                 value = value + got_b2[u][j, o]
-            for y in range(ny):
-                send_c[j, y, u] = value[y * cbp:(y + 1) * cbp]
-        for o in range(1, ny):
-            copy = remote(send_c.at[j, lax.rem(me_y + o, ny)], got_c.at[j, o - 1],
-                          sc.at[j, o - 1], rc.at[j, o - 1], at_y(o))
+            for y in range(ny // HALVES):
+                send_c[j, u * (ny // HALVES) + y] = value[y * cbp:(y + 1) * cbp]
+        for copy in c_copies(j):
             copy.start()
-            c_copies.setdefault(j, []).append(copy)
-            sent.append(copy)
 
     def finish(j):
-        for copy in c_copies.get(j, []):
+        for copy in c_copies(j):
             copy.wait_recv()
-        for u in range(HALVES):
-            value = send_c[j, me_y, u]
-            for o in range(ny - 1):
-                value = value + got_c[j, o, u]
-            out[j * HALVES + u] = (value * norm)[:, :mom]
+        value = send_c[j, me_y]
+        for o in range(ny - 1):
+            value = value + got_c[j, o]
+        out[j] = (value * norm)[:, :mom]
 
     compute(0)
     pl.semaphore_wait(barrier, len(partners))
     send_stage_a(0)
-    stages = (stage_b1, stage_b2, stage_c, finish)
-    for step in range(1, chunks + len(stages)):
-        if step < chunks:
+
+    @pl.loop(1, chunks + LAGS[-1])
+    def _(step):
+        @pl.when(step < chunks)
+        def _():
             compute(step)
             send_stage_a(step)
-        for depth, stage in enumerate(stages):
-            j = step - 1 - depth
-            if 0 <= j < chunks:
-                stage(j)
-    for copy in sent:
-        copy.wait_send()
+
+        for lag, stage in zip(LAGS, (stage_b1, stage_b2, stage_c, finish)):
+            pl.when((step >= lag) & (step < chunks + lag))(functools.partial(stage, step - lag))
+
+    @pl.loop(0, chunks)
+    def _(j):
+        for copy in a_copies(j) + c_copies(j):
+            copy.wait_send()
+        for u in range(HALVES):
+            for copy in b1_copies(j, u) + b2_copies(j, u):
+                copy.wait_send()
 
 
 def local(axis_sizes, correlators, momenta, source_channel, phase_code):
@@ -226,10 +233,10 @@
     nb = 2 if nx % 2 == 0 else 1
     na = nx // nb
     tpo = window // nx
-    chunks = tpo // HALVES
+    chunks = tpo
     cb = width // (ny * nz)
     cbp = round_up(cb, SUBLANES)
-    rows = ny * cbp
+    half_rows = ny * cbp // HALVES
     sites = cells_x * cells_y * cells_z
     lanes = round_up(mom, LANES)
     norm = 1.0 / math.sqrt(sites * nx * ny * nz)
@@ -254,14 +261,14 @@
     scratch = [
         pltpu.VMEM((window, sites, width), correlators.dtype),
         pltpu.VMEM((sites, 2 * lanes), jnp.bfloat16),
-        buffer(chunks, nz, HALVES, nx, rows, lanes),
-        buffer(chunks, less(nz), HALVES, nx, rows, lanes),
-        [buffer(chunks, less(lead[u]), trail[u], rows, lanes) for u in range(HALVES)],
-        [buffer(chunks, less(lead[u]), trail[u], rows, lanes) for u in range(HALVES)],
-        [buffer(chunks, less(trail[u]), rows, lanes) for u in range(HALVES)],
-        [buffer(chunks, less(trail[u]), rows, lanes) for u in range(HALVES)],
-        buffer(chunks, ny, HALVES, cbp, lanes),
-        buffer(chunks, less(ny), HALVES, cbp, lanes),
+        buffer(chunks, nz, HALVES, nx, half_rows, lanes),
+        buffer(chunks, less(nz), HALVES, nx, half_rows, lanes),
+        [buffer(chunks, less(lead[u]), trail[u], half_rows, lanes) for u in range(HALVES)],
+        [buffer(chunks, less(lead[u]), trail[u], half_rows, lanes) for u in range(HALVES)],
+        [buffer(chunks, less(trail[u]), half_rows, lanes) for u in range(HALVES)],
+        [buffer(chunks, less(trail[u]), half_rows, lanes) for u in range(HALVES)],
+        buffer(chunks, ny, cbp, lanes),
+        buffer(chunks, less(ny), cbp, lanes),
         sems(chunks, nx),
         sems(chunks, less(nz)),
         sems(chunks, less(nz)),

time: 27.3 us -> 27 us (0.989)
  Pallas kernels: 25.8 us -> 25.5 us
    pallas_call x1, Pallas kernels: 25.8 us -> 25.5 us  [local(): pl.pallas_call(functools.partial(kernel, dims), out_shape=jax.ShapeDtypeS...]
where the time goes in v3:
time: 27 us; the launch traced here: 26.8 us
  Pallas kernels  25.5 us (94%)
  other arithmetic  0.72 us (3%)
  local copies, waits for them, and re-layouts  0.63 us (2%)
    pallas_call x1, Pallas kernels, local(): pl.pallas_call(functools.partial(kernel, dims), out_shape=jax.ShapeDtypeS...  25.5 us
    add x1, other arithmetic, local(): sum((jnp.pad(row, ((at, SUBLANES - at - row.shape[0]), (0, small_lanes -...  0.72 us
    unnamed x1, local copies, waits for them, and re-layouts  0.63 us

profile of v3, /device:TPU:0, one launch (start us, length us, event | category | flops | bytes accessed | tf_op | source)
XLA Modules:
  0.0 26.8 jit_solution(11637619986771627753)
XLA Ops:
  0.0 0.7 %pad_add_fusion.small = s32[8,128]{1,0:T(8,128)S(1)} fusion(s32[1,64]{1,0:T(1,128)} %bitcast.8, s32[1,64]{1,0:T(1,128)} %bitcast.9, s32[3,125]{1,0:T(4,128)} %bitcast.7), kind=kLoop, calls=%fused_computation | loop fusion | flops 2048 | bytes 6108 | tf_op jit(solution)/shard_map/add | solution.py:246
  0.7 25.5 %project.1 = f32[8,16,125]{2,1,0:T(8,128)S(1)} custom-call(bf16[32,512,128]{2,1,0:T(8,128)(2,1)} %bitcast.6, s32[8,128]{1,0:T(8,128)S(1)} %pad_add_fusion.small), custom_call_target="tpu_custom_call" | custom-call | tf_op jit(solution)/shard_map/project/pallas_call | solution.py:283
  26.2 0.6 %copy.6 = f32[8,125,16]{1,2,0:T(8,128)} copy(f32[8,125,16]{1,2,0:T(8,128)S(1)} %bitcast.5) | data formatting | bytes 128000

commit v4 on v3

--- a/solution.py
+++ b/solution.py
@@ -11,7 +11,7 @@
 LANES = 128
 SUBLANES = 8
 HALVES = 2
-LAGS = (1, 4, 7, 10)
+LAGS = (1, 4, 8, 12)
 GROUP = 4
 
 

time: 27 us -> 26.9 us (level)
  no operation moved by 1% of the time
where the time goes in v4:
time: 26.9 us; the launch traced here: 26.7 us
  Pallas kernels  25.3 us (94%)
  other arithmetic  0.72 us (3%)
  local copies, waits for them, and re-layouts  0.63 us (2%)
    pallas_call x1, Pallas kernels, local(): pl.pallas_call(functools.partial(kernel, dims), out_shape=jax.ShapeDtypeS...  25.3 us
    add x1, other arithmetic, local(): sum((jnp.pad(row, ((at, SUBLANES - at - row.shape[0]), (0, small_lanes -...  0.72 us
    unnamed x1, local copies, waits for them, and re-layouts  0.63 us

profile of v4, /device:TPU:0, one launch (start us, length us, event | category | flops | bytes accessed | tf_op | source)
XLA Modules:
  0.0 26.7 jit_solution(1028275426877421242)
XLA Ops:
  0.0 0.7 %pad_add_fusion.small = s32[8,128]{1,0:T(8,128)S(1)} fusion(s32[1,64]{1,0:T(1,128)} %bitcast.8, s32[1,64]{1,0:T(1,128)} %bitcast.9, s32[3,125]{1,0:T(4,128)} %bitcast.7), kind=kLoop, calls=%fused_computation | loop fusion | flops 2048 | bytes 6108 | tf_op jit(solution)/shard_map/add | solution.py:246
  0.7 25.3 %project.1 = f32[8,16,125]{2,1,0:T(8,128)S(1)} custom-call(bf16[32,512,128]{2,1,0:T(8,128)(2,1)} %bitcast.6, s32[8,128]{1,0:T(8,128)S(1)} %pad_add_fusion.small), custom_call_target="tpu_custom_call" | custom-call | tf_op jit(solution)/shard_map/project/pallas_call | solution.py:283
  26.1 0.6 %copy.6 = f32[8,125,16]{1,2,0:T(8,128)} copy(f32[8,125,16]{1,2,0:T(8,128)S(1)} %bitcast.5) | data formatting | bytes 128000
